TPU v7x, 32 devices: a whole 2x2x4 slice. The times are simulated.
32 devices in a mesh: dp: 8 (over z, x), rep: 4 (over y, core).
Axes of the slice: x: 2, y: 2, z: 4, core: 2. Of those that a mesh axis runs over, the one named last changes fastest.
Arguments:
- features: bfloat16 [5120, 8192], P('dp', 'rep'), may hold values from -6 to 6
- out_grads: bfloat16 [5120, 1024], P('dp'), may hold values from -12 to 12, as said below
- cold_sums: bfloat16 [8, 8192, 1024], P('dp', 'rep'), may hold values from -96 to 96
- weight: float32 [8192, 1024], P(('rep', 'dp')), may hold values from -3 to 3
- moment: float32 [8192, 1024], P(('rep', 'dp')), may hold values from -6 to 6
- second: float32 [8192, 1024], P(('rep', 'dp')), may hold values from 0.01 to 4
- ranks: int32 [8], replicated, may hold values from 0 to 7, each once
Outputs:
- new_weight: float32 [8192, 1024], P(('rep', 'dp'))
- new_moment: float32 [8192, 1024], P(('rep', 'dp'))
- new_second: float32 [8192, 1024], P(('rep', 'dp'))
- new_cold: bfloat16 [8, 8192, 1024], P('dp', 'rep')
- column_sq: float32 [1024], replicated
Inputs may be any that keep to these rules, and one draw needn't show every extreme that they name: `ranks`: each block number appears once. `out_grads`: column scales differ from column to column.
All inputs are finite; a program needn't handle non-finite values.
Results may differ from a plain program's by a relative error of at most 0.001.
Values sent between devices are 32-bit elements; how exact they have to be, the bound alone decides.
A program may use at most 128 MiB of HBM per device.

v0:
```python
import jax
import jax.numpy as jnp
from jax import lax
from jax.sharding import PartitionSpec as P


def body(features, out_grads, cold_sums, weight, moment, second, ranks):
    blocks = ranks.shape[0]
    hot_count = blocks // 2
    width = out_grads.shape[1]
    local_rows = features.shape[1]
    grad = lax.dot_general(
        features, out_grads, (((0,), (0,)), ((), ())), preferred_element_type=jnp.float32
    )
    local = cold_sums[0].astype(jnp.float32) + grad
    hot_block = ranks < hot_count
    hot_col = jnp.repeat(hot_block, 128)
    new_cold = jnp.where(hot_col[None, :], jnp.float32(0.0), local).astype(jnp.bfloat16)[None]
    partial_sq = jnp.sum(local * local, axis=0)
    column_sq = lax.psum(partial_sq, ("dp", "rep"))
    picker = (ranks[None, :] == jnp.arange(hot_count, dtype=jnp.int32)[:, None]).astype(jnp.float32)
    packed = jnp.einsum(
        "rbk,sb->rsk",
        local.reshape(local_rows, blocks, 128),
        picker,
        precision=lax.Precision.HIGHEST,
    )
    owned = lax.psum_scatter(
        packed.reshape(local_rows, hot_count * 128), "dp", scatter_dimension=0, tiled=True
    )
    owned_rows = owned.shape[0]
    spread = jnp.einsum(
        "rsk,sb->rbk",
        owned.reshape(owned_rows, hot_count, 128),
        picker,
        precision=lax.Precision.HIGHEST,
    )
    summed = spread.reshape(owned_rows, width)
    dp_count = lax.axis_size("dp")
    total_rows = local_rows * lax.axis_size("rep")
    rms = jnp.sqrt(column_sq / jnp.float32(total_rows * dp_count * features.shape[0]))
    clip = 1.0 / jnp.maximum(jnp.float32(1.0), rms)
    grad_mean = summed * clip[None, :] / jnp.float32(dp_count)
    moved = 0.9 * moment + 0.1 * grad_mean
    squared = 0.95 * second + 0.05 * grad_mean * grad_mean
    step_size = 0.05 * (moved / (1.0 - 0.9**10)) / (jnp.sqrt(squared / (1.0 - 0.95**10)) + 1e-08)
    new_moment = jnp.where(hot_col[None, :], moved, moment)
    new_second = jnp.where(hot_col[None, :], squared, second)
    new_weight = jnp.where(hot_col[None, :], weight - step_size, weight)
    return (new_weight, new_moment, new_second, new_cold, column_sq)


def solution(mesh):
    placed = (
        P("dp", "rep"),
        P("dp", None),
        P("dp", "rep", None),
        P(("rep", "dp"), None),
        P(("rep", "dp"), None),
        P(("rep", "dp"), None),
        P(),
    )
    return jax.shard_map(
        body,
        mesh=mesh,
        in_specs=placed,
        out_specs=(
            P(("rep", "dp"), None),
            P(("rep", "dp"), None),
            P(("rep", "dp"), None),
            P("dp", "rep", None),
            P(),
        ),
        check_vma=False,
    )
```

profile of v0, /device:TPU:0, one launch (start us, length us, event | category | flops | bytes accessed | tf_op | source)
XLA Modules:
  0.0 146.8 jit_solution(3876229552257421479)
XLA Ops:
  7.2 0.0 copy-start
  7.2 0.0 reduce-scatter.2.cloned.1.call-start
  7.2 6.6 %copy.12 = bf16[1,2048,1024]{1,2,0:T(8,128)(2,1)} copy(bf16[1,2048,1024]{2,1,0:T(8,128)(2,1)} %param.9) | data formatting | bytes 8388608 | tf_op args[2]
  13.8 0.0 copy-done
  13.8 8.0 %multiply_reduce_fusion = (f32[1024]{0:T(1024)S(1)}, f32[2048,1024]{0,1:T(8,128)}) fusion(bf16[640,2048]{1,0:T(8,128)(2,1)S(1)} %copy-done, bf16[640,1024]{1,0:T(8,128)(2,1)} %param.8, bf16[1,2048,1024]{1,2,0:T(8,128)(2,1)} %copy.12), kind=kOutput, calls=%fused_computation.2 | convolution fusion | flops 2692742144 | bytes 16519168 | tf_op jit(solution)/shard_map/dot_general | solution.py:12
  21.8 0.0 copy-start.2
  21.8 9.3 %copy.13 = f32[2048,8,128]{2,1,0:T(8,128)} copy(f32[2048,8,128]{0,2,1:T(8,128)} %bitcast.37) | data formatting | bytes 16777216 | tf_op jit(solution)/shard_map/reshape | solution.py:24
  31.1 0.0 copy-done.2
  31.1 7.4 %fusion.6 = f32[4,2048,128]{2,0,1:T(4,128)S(1)} fusion(f32[2048,8,128]{2,1,0:T(8,128)} %copy.13, s32[8]{0:T(128)S(1)} %copy-done.2), kind=kOutput, calls=%fused_computation.16 | convolution fusion | flops 100663328 | bytes 12582944 | tf_op jit(solution)/shard_map/rbk,sb->rsk/dot_general | solution.py:22
  38.6 2.4 %copy.31 = f32[256,8,4,128]{3,1,2,0:T(8,128)} copy(f32[256,8,4,128]{3,2,1,0:T(4,128)S(1)} %bitcast.39) | data formatting | bytes 8388608
  41.0 0.0 reduce-scatter.2.cloned.1.call-update
  41.0 0.1 broadcast_bitcast_fusion
  41.1 5.9 %fusion = bf16[1,2048,1024]{1,2,0:T(8,128)(2,1)} fusion(f32[2048,1024]{0,1:T(8,128)} %get-tuple-element.14, pred[1024]{0:T(1024)(128)(4,1)S(1)} %broadcast_bitcast_fusion), kind=kLoop, calls=%fused_computation.3 | loop fusion | flops 2097152 | bytes 12583936 | tf_op jit(solution)/shard_map/broadcast_in_dim | solution.py:18
  47.0 6.4 %copy.14 = bf16[1,2048,1024]{2,1,0:T(8,128)(2,1)} copy(bf16[1,2048,1024]{1,2,0:T(8,128)(2,1)} %fusion) | data formatting | bytes 8388608
  53.4 43.8 %psum.7 = f32[1024]{0:T(1024)S(1)} all-reduce(f32[1024]{0:T(1024)S(1)} %get-tuple-element.13), channel_id=1, replica_groups=mesh['dp'=8,'rep'=4] {'dp','rep'}, use_global_device_ids=true, to_apply=%region_2.3 | all-reduce | flops 1024 | bytes 8192 | tf_op jit(solution)/shard_map/psum | solution.py:20
  97.2 0.0 copy-start.1
  97.2 36.1 %reduce-scatter.2.cloned.1.call-done = f32[256,512]{1,0:T(8,128)} async-done(((f32[2048,512]{1,0:T(8,128)}), f32[256,512]{1,0:T(8,128)}) %reduce-scatter.2.cloned.1.call-update) | async-done | bytes 524304 | tf_op jit(solution)/shard_map/reduce_scatter | solution.py:28
  133.3 1.2 reshape.29
  134.5 0.7 fusion.4
  135.3 4.6 %fusion.2 = (f32[256,1024]{1,0:T(8,128)}, f32[256,1024]{1,0:T(8,128)}, f32[256,1024]{1,0:T(8,128)}) fusion(f32[256,1024]{1,0:T(8,128)} %param.12, f32[32,8,8,128]{3,2,1,0:T(8,128)S(1)} %bitcast.40, f32[1024]{0:T(1024)S(1)} %maximum_divide_fusion, pred[1024]{0:T(1024)(128)(4,1)S(1)} %broadcast_bitcast_fusion, f32[256,1024]{1,0:T(8,128)} %param.10, ...), kind=kLoop, calls=%fused_computation.10 | loop fusion | flops 4456448 | bytes 7345152 | tf_op jit(solution)/shard_map/jit(_where)/select_n | solution.py:48
  139.9 0.0 copy-done.1
  (2 shorter events, 0.0 us)
Async XLA Ops:
  7.2 6.6 %copy-start = (bf16[640,2048]{1,0:T(8,128)(2,1)S(1)}, bf16[640,2048]{1,0:T(8,128)(2,1)}, u32[]{:S(2)}) copy-start(bf16[640,2048]{1,0:T(8,128)(2,1)} %param.7) | copy-start | bytes 7864324
  7.2 126.1 %reduce-scatter.2.cloned.1.call-start = ((), (), s32[]{:S(2)}) async-start(), calls=%async_computation.1 | async-start | bytes 4718592 | tf_op jit(solution)/shard_map/reduce_scatter | solution.py:28
  21.8 9.3 %copy-start.2 = (s32[8]{0:T(128)S(1)}, s32[8]{0:T(128)}, u32[]{:S(2)}) copy-start(s32[8]{0:T(128)} %param.13) | copy-start | bytes 100
  97.2 42.7 %copy-start.1 = (f32[1024]{0:T(1024)}, f32[1024]{0:T(1024)S(1)}, u32[]{:S(2)}) copy-start(f32[1024]{0:T(1024)S(1)} %psum.7) | copy-start | bytes 12292
Sparse Core Ops, SparseCore 0:
  41.1 92.1 reduce-scatter.1
where the time goes:
time: 147 us
  blocking collectives  43.8 us (30%)
  waiting for transfers between devices  36.1 us (25%)
  local copies, waits for them, and re-layouts  26 us (18%)
  matrix products  16.2 us (11%)
  between operations  14.1 us (10%)
  other arithmetic  10.5 us (7%)
    psum x1, blocking collectives, body(): column_sq = lax.psum(partial_sq, ('dp', 'rep'))  43.8 us
    reduce_scatter x1, waiting for transfers between devices, body(): lax.psum_scatter(packed.reshape(local_rows, hot_count * 128), 'dp', scatt...  36.1 us
    unnamed x9, local copies, waits for them, and re-layouts  15.4 us
    reshape x1, local copies, waits for them, and re-layouts, body(): local.reshape(local_rows, blocks, 128)  9.3 us
    dot_general x1, matrix products, body(): lax.dot_general(features, out_grads, (((0,), (0,)), ((), ())), preferred_...  8.02 us
    dot_general x1, matrix products, body(): jnp.einsum('rbk,sb->rsk', local.reshape(local_rows, blocks, 128), picker,...  7.42 us
    broadcast_in_dim x1, other arithmetic, body(): jnp.where(hot_col[None, :], jnp.float32(0.0), local).astype(jnp.bfloat16)  5.88 us
    select_n x1, other arithmetic, body(): new_second = jnp.where(hot_col[None, :], squared, second)  4.64 us
  transfers between devices with their start and end apart: 1, of which 1 were waited for; matrix products, arithmetic and copies ran while one was open for 8% of the time, Pallas kernels for 0%

commit v1 on v0

--- a/solution.py
+++ b/solution.py
@@ -17,7 +17,7 @@
     hot_col = jnp.repeat(hot_block, 128)
     new_cold = jnp.where(hot_col[None, :], jnp.float32(0.0), local).astype(jnp.bfloat16)[None]
     partial_sq = jnp.sum(local * local, axis=0)
-    column_sq = lax.psum(partial_sq, ("dp", "rep"))
+    column_sq = jnp.sum(lax.all_gather(partial_sq, ("dp", "rep")), axis=0)
     picker = (ranks[None, :] == jnp.arange(hot_count, dtype=jnp.int32)[:, None]).astype(jnp.float32)
     packed = jnp.einsum(
         "rbk,sb->rsk",

time: 147 us -> 147 us (level)
  waiting for transfers between devices: 36.1 us -> 33.7 us
  blocking collectives: 43.8 us -> 45.4 us
    all_gather x0 -> x1, blocking collectives: none -> 45.4 us  [body(): column_sq = jnp.sum(lax.all_gather(partial_sq, ('dp', 'rep')), axis=0)]
    psum x1 -> x0, blocking collectives: 43.8 us -> none  [body(): column_sq = lax.psum(partial_sq, ('dp', 'rep'))]
    reduce_scatter x1, waiting for transfers between devices: 36.1 us -> 33.7 us  [body(): lax.psum_scatter(packed.reshape(local_rows, hot_count * 128), 'dp', scatt...]
  transfers between devices with their start and end apart: 1 -> 1, of which waited for: 1 -> 1; matrix products, arithmetic and copies ran while one was open for 8% -> 9% of each run, Pallas kernels for 0% -> 0%
where the time goes in v1:
time: 147 us; the launch traced here: 146 us
  blocking collectives  45.4 us (31%)
  waiting for transfers between devices  33.7 us (23%)
  local copies, waits for them, and re-layouts  26 us (18%)
  matrix products  16.2 us (11%)
  between operations  14.1 us (10%)
  other arithmetic  10.7 us (7%)
    all_gather x1, blocking collectives, body(): column_sq = jnp.sum(lax.all_gather(partial_sq, ('dp', 'rep')), axis=0)  45.4 us
    reduce_scatter x1, waiting for transfers between devices, body(): lax.psum_scatter(packed.reshape(local_rows, hot_count * 128), 'dp', scatt...  33.7 us
    unnamed x9, local copies, waits for them, and re-layouts  15.4 us
    reshape x1, local copies, waits for them, and re-layouts, body(): local.reshape(local_rows, blocks, 128)  9.3 us
    dot_general x1, matrix products, body(): lax.dot_general(features, out_grads, (((0,), (0,)), ((), ())), preferred_...  8.02 us
    dot_general x1, matrix products, body(): jnp.einsum('rbk,sb->rsk', local.reshape(local_rows, blocks, 128), picker,...  7.42 us
    broadcast_in_dim x1, other arithmetic, body(): jnp.where(hot_col[None, :], jnp.float32(0.0), local).astype(jnp.bfloat16)  6.03 us
    select_n x1, other arithmetic, body(): new_second = jnp.where(hot_col[None, :], squared, second)  4.64 us
  transfers between devices with their start and end apart: 1, of which 1 were waited for; matrix products, arithmetic and copies ran while one was open for 9% of the time, Pallas kernels for 0%

profile of v1, /device:TPU:0, one launch (start us, length us, event | category | flops | bytes accessed | tf_op | source)
XLA Modules:
  0.0 146.1 jit_solution(11470997553850710658)
XLA Ops:
  7.2 0.0 copy-start
  7.2 0.0 reduce-scatter.2.cloned.1.call-start
  7.2 6.6 %copy.18 = bf16[1,2048,1024]{1,2,0:T(8,128)(2,1)} copy(bf16[1,2048,1024]{2,1,0:T(8,128)(2,1)} %param.9) | data formatting | bytes 8388608 | tf_op args[2]
  13.8 0.0 copy-done
  13.8 8.0 %multiply_reduce_fusion = (f32[1024]{0:T(1024)S(1)}, f32[2048,1024]{0,1:T(8,128)}) fusion(bf16[640,2048]{1,0:T(8,128)(2,1)S(1)} %copy-done, bf16[640,1024]{1,0:T(8,128)(2,1)} %param.8, bf16[1,2048,1024]{1,2,0:T(8,128)(2,1)} %copy.18), kind=kOutput, calls=%fused_computation.2 | convolution fusion | flops 2692742144 | bytes 16519168 | tf_op jit(solution)/shard_map/dot_general | solution.py:12
  21.8 0.0 copy-start.2
  21.8 9.3 %copy.19 = f32[2048,8,128]{2,1,0:T(8,128)} copy(f32[2048,8,128]{0,2,1:T(8,128)} %bitcast.37) | data formatting | bytes 16777216 | tf_op jit(solution)/shard_map/reshape | solution.py:24
  31.1 0.0 copy-done.2
  31.1 7.4 %fusion.6 = f32[4,2048,128]{2,0,1:T(4,128)S(1)} fusion(f32[2048,8,128]{2,1,0:T(8,128)} %copy.19, s32[8]{0:T(128)S(1)} %copy-done.2), kind=kOutput, calls=%fused_computation.16 | convolution fusion | flops 100663328 | bytes 12582944 | tf_op jit(solution)/shard_map/rbk,sb->rsk/dot_general | solution.py:22
  38.6 2.4 %copy.37 = f32[256,8,4,128]{3,1,2,0:T(8,128)} copy(f32[256,8,4,128]{3,2,1,0:T(4,128)S(1)} %bitcast.39) | data formatting | bytes 8388608
  41.0 0.0 reduce-scatter.2.cloned.1.call-update
  41.0 45.4 %all-gather = f32[32768]{0:T(1024)S(1)} all-gather(f32[1024]{0:T(1024)S(1)} %get-tuple-element.23), channel_id=2, replica_groups=mesh['dp'=8,'rep'=4] {'dp','rep'}, dimensions={0}, use_global_device_ids=true | all-gather | bytes 135168 | tf_op jit(solution)/shard_map/all_gather | solution.py:20
  86.4 0.1 broadcast_bitcast_fusion
  86.5 6.0 %fusion = bf16[1,2048,1024]{1,2,0:T(8,128)(2,1)} fusion(f32[2048,1024]{0,1:T(8,128)} %get-tuple-element.24, pred[1024]{0:T(1024)(128)(4,1)S(1)} %broadcast_bitcast_fusion), kind=kLoop, calls=%fused_computation.3 | loop fusion | flops 2097152 | bytes 12583936 | tf_op jit(solution)/shard_map/broadcast_in_dim | solution.py:18
  92.5 6.4 %copy.20 = bf16[1,2048,1024]{2,1,0:T(8,128)(2,1)} copy(bf16[1,2048,1024]{1,2,0:T(8,128)(2,1)} %fusion) | data formatting | bytes 8388608
  99.0 0.0 copy-start.1
  99.0 33.7 %reduce-scatter.2.cloned.1.call-done = f32[256,512]{1,0:T(8,128)} async-done(((f32[2048,512]{1,0:T(8,128)}), f32[256,512]{1,0:T(8,128)}) %reduce-scatter.2.cloned.1.call-update) | async-done | bytes 524304 | tf_op jit(solution)/shard_map/reduce_scatter | solution.py:28
  132.7 1.2 reshape.34
  133.9 0.7 fusion.4
  134.6 4.6 %fusion.2 = (f32[256,1024]{1,0:T(8,128)}, f32[256,1024]{1,0:T(8,128)}, f32[256,1024]{1,0:T(8,128)}) fusion(f32[256,1024]{1,0:T(8,128)} %param.12, f32[32,8,8,128]{3,2,1,0:T(8,128)S(1)} %bitcast.40, f32[1024]{0:T(1024)S(1)} %maximum_divide_fusion, pred[1024]{0:T(1024)(128)(4,1)S(1)} %broadcast_bitcast_fusion, f32[256,1024]{1,0:T(8,128)} %param.10, ...), kind=kLoop, calls=%fused_computation.10 | loop fusion | flops 4456448 | bytes 7345152 | tf_op jit(solution)/shard_map/jit(_where)/select_n | solution.py:48
  139.3 0.0 copy-done.1
  (4 shorter events, 0.1 us)
Async XLA Ops:
  7.2 6.6 %copy-start = (bf16[640,2048]{1,0:T(8,128)(2,1)S(1)}, bf16[640,2048]{1,0:T(8,128)(2,1)}, u32[]{:S(2)}) copy-start(bf16[640,2048]{1,0:T(8,128)(2,1)} %param.7) | copy-start | bytes 7864324
  7.2 125.5 %reduce-scatter.2.cloned.1.call-start = ((), (), s32[]{:S(2)}) async-start(), calls=%async_computation.1 | async-start | bytes 4718592 | tf_op jit(solution)/shard_map/reduce_scatter | solution.py:28
  21.8 9.3 %copy-start.2 = (s32[8]{0:T(128)S(1)}, s32[8]{0:T(128)}, u32[]{:S(2)}) copy-start(s32[8]{0:T(128)} %param.13) | copy-start | bytes 100
  99.0 40.3 %copy-start.1 = (f32[1024]{0:T(1024)}, f32[1024]{0:T(1024)S(1)}, u32[]{:S(2)}) copy-start(f32[1024]{0:T(1024)S(1)} %reduce_sum.19) | copy-start | bytes 12292
Sparse Core Ops, SparseCore 0:
  41.1 91.5 reduce-scatter.1
